TPU v7x, 32 devices: a whole 2x2x4 slice. The times are simulated.
32 devices in a mesh: inp: 8 (over z, y), tm: 4 (over x, core).
Axes of the slice: x: 2, y: 2, z: 4, core: 2. Of those that a mesh axis runs over, the one named last changes fastest.
Arguments:
- voltages: bfloat16 [1024, 262144], P('inp', 'tm'), may hold values from -6 to 6
- pfb_coeff: float32 [16, 512], replicated, may hold values from -1.5 to 1.5
Outputs:
- visibilities: float32 [32, 2, 1024, 1024], P(('inp', 'tm'))
All inputs are finite; a program needn't handle non-finite values.
Results may differ from a plain program's by a relative error of at most 0.0029.
Values may be sent and summed in bfloat16 or wider, within the bound.
A program may use at most 128 MiB of HBM per device.

v0:
```python
import math

import jax
import jax.numpy as jnp
from jax import lax
from jax.sharding import PartitionSpec as P

CH_DEV = 1


def shifted(block, axis, distance):
    devices = range(lax.axis_size(axis))
    route = [(i - distance, i) for i in devices if i - distance in devices]
    return lax.ppermute(block, axis, route)


def dft_rows(channel_ids, length):
    samples = jnp.arange(length, dtype=jnp.int32)
    phase_index = channel_ids[:, None] * samples[None, :] % length
    phase_angle = phase_index.astype(jnp.float32) * (2.0 * math.pi / length)
    norm_scale = 1.0 / math.sqrt(length)
    cos_part = jnp.cos(phase_angle) * norm_scale
    sin_part = -jnp.sin(phase_angle) * norm_scale
    return jnp.stack([cos_part, sin_part], axis=1).reshape(2 * channel_ids.shape[0], length)


def correlate(received):
    item_count = received.shape[1]
    inputs_all = received.shape[3]
    spectra_all = received.shape[4]
    stacked = received.reshape(item_count, 2 * inputs_all, spectra_all)
    products = jnp.einsum("kas,kbs->kab", stacked, stacked, preferred_element_type=jnp.float32)
    real_sum = products[:, :inputs_all, :inputs_all] + products[:, inputs_all:, inputs_all:]
    imag_diff = products[:, inputs_all:, :inputs_all] - products[:, :inputs_all, inputs_all:]
    return jnp.stack([real_sum, imag_diff], axis=1) * (1.0 / spectra_all)


def per_device(voltages, pfb_coeff):
    in_rows = voltages.shape[0]
    tap_count = pfb_coeff.shape[0]
    length = pfb_coeff.shape[1]
    spec_dev = voltages.shape[1] // length
    groups_inp = lax.axis_size("inp")
    groups_tm = lax.axis_size("tm")
    channels = CH_DEV * groups_inp * groups_tm
    blocks = voltages.reshape(in_rows, spec_dev, length)
    tail_blocks = blocks[:, spec_dev - (tap_count - 1) :, :]
    history = shifted(tail_blocks, "tm", 1)
    extended = jnp.concatenate([history, blocks], axis=1)
    filtered = jnp.zeros((in_rows, spec_dev, length), jnp.float32)
    for tap_index in range(tap_count):
        filtered = filtered + pfb_coeff[tap_index][None, None, :] * extended[
            :, tap_index : tap_index + spec_dev, :
        ].astype(jnp.float32)
    positions = jnp.arange(channels, dtype=jnp.int32)
    dft_table = dft_rows(positions, length)
    spectra = jnp.einsum(
        "cn,asn->cas",
        dft_table,
        filtered,
        precision=lax.Precision.HIGHEST,
        preferred_element_type=jnp.float32,
    ).astype(jnp.bfloat16)
    outgoing = spectra.reshape(groups_inp, 2 * channels // groups_inp, in_rows, spec_dev)
    turned = lax.all_to_all(outgoing, "inp", split_axis=0, concat_axis=2, tiled=True)
    per_slab = turned.reshape(groups_tm, CH_DEV, 2, in_rows * groups_inp, spec_dev)
    result = correlate(lax.all_to_all(per_slab, "tm", split_axis=0, concat_axis=4, tiled=True))
    return result


def solution(mesh):
    return jax.shard_map(
        per_device,
        mesh=mesh,
        in_specs=(P("inp", "tm"), P()),
        out_specs=P(("inp", "tm"), None, None, None),
        check_vma=False,
    )
```

profile of v0, /device:TPU:0, one launch (start us, length us, event | category | flops | bytes accessed | tf_op | source)
XLA Modules:
  0.0 309.1 jit_solution(6881728016254690156)
XLA Ops:
  0.0 0.0 copy-start
  0.0 22.4 %copy.27 = bf16[128,65536]{0,1:T(8,128)(2,1)} copy(bf16[128,65536]{1,0:T(8,128)(2,1)} %param.2) | data formatting | bytes 33554432 | tf_op args[0]
  22.4 1.7 slice.144
  24.1 2.3 copy.28
  26.4 3.7 %collective-permute-start = (bf16[128,15,512]{2,0,1:T(8,128)(2,1)}, bf16[128,15,512]{2,0,1:T(8,128)(2,1)}, u32[]{:S(2)}, u32[]{:S(2)}) collective-permute-start(bf16[128,15,512]{2,0,1:T(8,128)(2,1)} %copy.28), channel_id=1, source_target_pairs={{0,1},{1,2},{2,3},{4,5},{5,6},{6,7},{8,9},{9,10},{10,11},{12,13},{... | collective-permute-start | bytes 5898248 | tf_op jit(solution)/shard_map/ppermute | solution.py:14
  30.0 0.3 negate_multiply_fusion
  30.3 0.1 copy.26
  30.4 0.1 reshape.154
  30.5 0.0 copy-done
  30.6 2.1 collective-permute-done
  32.7 2.8 copy.29
  35.5 91.2 %multiply_add_fusion = f32[128,128,512]{0,2,1:T(8,128)} fusion(bf16[128,128,512]{0,2,1:T(8,128)(2,1)} %bitcast.43, bf16[128,15,512]{0,2,1:T(8,128)(2,1)S(1)} %copy.29, f32[512]{0:T(512)S(1)} %bitcast.61, f32[512]{0:T(512)S(1)} %bitcast.62, f32[512]{0:T(512)S(1)} %bitcast.48, f32[512]{0:T(512)S(1)} %bitcast.49, f32[512]{0:T(512)S(1)} %bitcast.50, ...), kind=kLoop, calls=%fused_computation.14 | loop fusion | flops 520093696 | bytes 52330496 | tf_op jit(solution)/shard_map/add | solution.py:52
  126.7 34.6 %copy.30 = f32[128,128,512]{2,1,0:T(8,128)} copy(f32[128,128,512]{0,2,1:T(8,128)} %multiply_add_fusion) | data formatting | bytes 67108864 | tf_op jit(solution)/shard_map/add | solution.py:52
  161.3 35.3 %convert_bitcast_fusion = bf16[8,8,128,128]{3,1,0,2:T(8,128)(2,1)S(1)} fusion(f32[64,512,1]{1,0,2:T(8,128)S(1)} %reshape.154, f32[128,128,512]{2,1,0:T(8,128)} %copy.30), kind=kOutput, calls=%fused_computation.46 | convolution fusion | flops 6443499520 | bytes 35782656 | tf_op jit(solution)/shard_map/cn,asn->cas/dot_general | solution.py:57
  196.6 1.4 copy.31
  198.0 49.0 %all_to_all.30 = bf16[8,8,128,128]{3,2,1,0:T(8,128)(2,1)S(1)} all-to-all(bf16[8,8,128,128]{3,2,1,0:T(8,128)(2,1)S(1)} %copy.31), channel_id=1, replica_groups=mesh['inp'=8,'tm'=4] {'inp'}, dimensions={0} | all-to-all | bytes 4194304 | tf_op jit(solution)/shard_map/all_to_all | solution.py:65
  246.9 0.2 copy.32
  247.2 34.8 %all_to_all.31 = bf16[4,1,2,1024,128]{4,3,2,1,0:T(8,128)(2,1)S(1)} all-to-all(bf16[4,1,2,1024,128]{4,3,2,1,0:T(8,128)(2,1)S(1)} %bitcast.44), channel_id=1, replica_groups=mesh['inp'=8,'tm'=4] {'tm'}, dimensions={0} | all-to-all | bytes 4194304 | tf_op jit(solution)/shard_map/all_to_all | solution.py:67
  281.9 1.6 copy.34
  283.5 8.3 %convolution_bitcast_fusion = f32[1,2048,2048]{2,1,0:T(8,128)} fusion(bf16[256,8,4,128]{3,2,1,0:T(4,128)(2,1)S(1)} %bitcast.46), kind=kOutput, calls=%fused_computation.38 | convolution fusion | flops 4294967296 | bytes 18874368 | tf_op jit(solution)/shard_map/kas,kbs->kab/dot_general | solution.py:32
  291.8 10.3 %fusion.15 = (f32[1,1,1024,1024]{3,2,1,0:T(8,128)S(1)}, f32[1,1,1024,1024]{3,2,1,0:T(8,128)}) fusion(f32[1,2048,2048]{2,1,0:T(8,128)} %convolution_bitcast_fusion), kind=kLoop, calls=%fused_computation.43 | loop fusion | flops 2097152 | bytes 25165824 | tf_op jit(solution)/shard_map/stack | solution.py:35
  302.1 7.0 %maximum_multiply_fusion = f32[1,2,1024,1024]{3,2,1,0:T(8,128)} fusion(f32[1,1,1024,1024]{3,2,1,0:T(8,128)} %get-tuple-element.6, f32[1,1,1024,1024]{3,2,1,0:T(8,128)S(1)} %get-tuple-element.5), kind=kLoop, calls=%fused_computation.39 | loop fusion | flops 4194304 | bytes 16777216 | tf_op jit(solution)/shard_map/mul | solution.py:35
  (2 shorter events, 0.0 us)
Async XLA Ops:
  0.0 30.5 %copy-start = (f32[16,512]{1,0:T(8,128)S(1)}, f32[16,512]{1,0:T(8,128)}, u32[]{:S(2)}) copy-start(f32[16,512]{1,0:T(8,128)} %param.3) | copy-start | bytes 98308
  26.4 6.3 %collective-permute-start = (bf16[128,15,512]{2,0,1:T(8,128)(2,1)}, bf16[128,15,512]{2,0,1:T(8,128)(2,1)}, u32[]{:S(2)}, u32[]{:S(2)}) collective-permute-start(bf16[128,15,512]{2,0,1:T(8,128)(2,1)} %copy.28), channel_id=1, source_target_pairs={{0,1},{1,2},{2,3},{4,5},{5,6},{6,7},{8,9},{9,10},{10,11},{12,13},{... | collective-permute-start | bytes 5898248 | tf_op jit(solution)/shard_map/ppermute | solution.py:14
where the time goes:
time: 310 us; the launch traced here: 309 us
  other arithmetic  109 us (35%)
  blocking collectives  83.7 us (27%)
  local copies, waits for them, and re-layouts  67.2 us (22%)
  matrix products  43.5 us (14%)
  starting transfers between devices  3.69 us (1%)
    add x1, other arithmetic, per_device(): filtered + pfb_coeff[tap_index][None, None, :] * extended[:, tap_index:ta...  91.2 us
    all_to_all x1, blocking collectives, per_device(): lax.all_to_all(outgoing, 'inp', split_axis=0, concat_axis=2, tiled=True)  49 us
    dot_general x1, matrix products, per_device(): jnp.einsum('cn,asn->cas', dft_table, filtered, precision=lax.Precision.HI...  35.3 us
    all_to_all x1, blocking collectives, per_device(): lax.all_to_all(per_slab, 'tm', split_axis=0, concat_axis=4, tiled=True)  34.8 us
    add x1, local copies, waits for them, and re-layouts, per_device(): filtered + pfb_coeff[tap_index][None, None, :] * extended[:, tap_index:ta...  34.6 us
    unnamed x3, local copies, waits for them, and re-layouts  22.4 us
    another operation x1, other arithmetic, correlate(): return jnp.stack([real_sum, imag_diff], axis=1) * (1.0 / spectra_all)  10.3 us
    dot_general x1, matrix products, correlate(): jnp.einsum('kas,kbs->kab', stacked, stacked, preferred_element_type=jnp.f...  8.28 us
  transfers between devices with their start and end apart: 1, of which 1 were waited for; matrix products, arithmetic and copies ran while one was open for 0% of the time, Pallas kernels for 0%

commit v1 on v0

v1 whole, which is shorter than its diff:
```python
import functools
import math

import jax
import jax.numpy as jnp
import numpy as np
from jax import lax
from jax.experimental import pallas as pl
from jax.experimental.pallas import tpu as pltpu
from jax.sharding import PartitionSpec as P

LANES = 128
ROWS = 16
GROUP = 8
CHUNK = 16
NT = (((1,), (1,)), ((), ()))


def dft_tables(channels, length):
    phase = np.arange(channels)[:, None] * np.arange(length)[None, :] % length
    angle = phase * (2.0 * math.pi / length)
    table = np.stack([np.cos(angle), -np.sin(angle)], axis=1) / math.sqrt(length)
    table = table.reshape(2 * channels, length).astype(np.float32)
    high = table.astype(jnp.bfloat16)
    low = (table - high.astype(np.float32)).astype(jnp.bfloat16)
    return np.concatenate([high, low], axis=0)


def channelize_kernel(
    n_inp, n_tm, volt, coef_in, table, out,
    slab, coef, f_high, f_low, stage, send,
    load_sem, tail_send, tail_recv, send_sem, recv_sem,
):
    in_rows = volt.shape[0]
    taps, length = coef_in.shape
    spec = volt.shape[1] // length
    lines = stage.shape[0] // CHUNK
    n_dev = n_inp * n_tm
    chunks = spec // CHUNK
    tail = (taps - 1) * length
    width = CHUNK * length
    a_tiles = in_rows // ROWS
    inp = lax.axis_index("inp")
    tm = lax.axis_index("tm")
    me = inp * n_tm + tm

    def load(q):
        return pltpu.make_async_copy(
            volt.at[:, pl.ds(pl.multiple_of(q * width, width), width)],
            slab.at[:, pl.ds(pl.multiple_of(tail + q * width, length), width)],
            load_sem.at[q],
        )

    for q in range(chunks):
        load(q).start()

    barrier = pltpu.get_barrier_semaphore()

    def greet(d, _):
        other = lax.rem(me + d, n_dev)
        pl.semaphore_signal(
            barrier, inc=1, device_id=(other // n_tm, lax.rem(other, n_tm)),
            device_id_type=pl.DeviceIdType.MESH,
        )
        return _

    lax.fori_loop(1, n_dev, greet, 0)
    for j in range(taps):
        coef[j] = jnp.broadcast_to(coef_in[j : j + 1, :], (8, length))
    pl.semaphore_wait(barrier, n_dev - 1)

    history = pltpu.make_async_remote_copy(
        src_ref=volt.at[:, pl.ds(spec * length - tail, tail)],
        dst_ref=slab.at[:, pl.ds(0, tail)],
        send_sem=tail_send, recv_sem=tail_recv,
        device_id=(inp, lax.rem(tm + 1, n_tm)),
        device_id_type=pl.DeviceIdType.MESH,
    )

    @pl.when(tm < n_tm - 1)
    def _():
        history.start()

    @pl.when(tm == 0)
    def _():
        def clear(e, _):
            slab[:, pl.ds(pl.multiple_of(e * length, length), length)] = jnp.zeros(
                (in_rows, length), slab.dtype
            )
            return _

        lax.fori_loop(0, taps - 1, clear, 0)

    def fir(first, tile, slot):
        row = pl.multiple_of(tile * ROWS, ROWS)
        for nt in range(length // LANES):
            lanes = pl.ds(nt * LANES, LANES)
            c = [coef[j, :, lanes] for j in range(taps)]
            low = [None] * GROUP
            high = [None] * GROUP
            for t in range(GROUP + taps - 1):
                col = pl.multiple_of((first + t) * length + nt * LANES, LANES)
                x = slab[pl.ds(row, ROWS), pl.ds(col, LANES)].astype(jnp.float32)
                x0, x1 = x[:8], x[8:]
                for i in range(max(0, t - taps + 1), min(GROUP - 1, t) + 1):
                    w = c[t - i]
                    if t == i:
                        low[i], high[i] = w * x0, w * x1
                    else:
                        low[i], high[i] = low[i] + w * x0, high[i] + w * x1
                i = t - taps + 1
                if i >= 0:
                    f = jnp.concatenate([low[i], high[i]], axis=0)
                    h = f.astype(jnp.bfloat16)
                    f_high[slot, i, pl.ds(row, ROWS), lanes] = h
                    f_low[slot, i, pl.ds(row, ROWS), lanes] = (
                        f - h.astype(jnp.float32)
                    ).astype(jnp.bfloat16)

    def dft(tile, slot):
        per = GROUP // a_tiles
        for u in range(per):
            i = tile * per + u
            r = lax.dot_general(table[...], f_high[slot, i], NT, preferred_element_type=jnp.float32)
            r2 = lax.dot_general(table[:lines], f_low[slot, i], NT, preferred_element_type=jnp.float32)
            stage[pl.ds(slot * GROUP + i, lines, stride=CHUNK), :] = r[:lines] + r[lines:] + r2

    def each(body):
        def step(tile, _):
            body(tile)
            return _

        lax.fori_loop(0, a_tiles, step, 0)

    def own(q):
        return pltpu.make_async_copy(send.at[q, me], place(out, q), recv_sem)

    def place(ref, q):
        first = pl.multiple_of(tm * spec + q * CHUNK, CHUNK)
        return ref.at[inp, :, pl.ds(first, CHUNK), :]

    def dispatch(q):
        def convert(d, _):
            rows = pl.ds(pl.multiple_of(d * 2 * CHUNK, 2 * CHUNK), 2 * CHUNK)
            send[q, d] = stage[rows, :].reshape(2, CHUNK, in_rows).astype(send.dtype)
            return _

        lax.fori_loop(0, n_dev, convert, 0)

        def post(d, _):
            other = lax.rem(me + d, n_dev)
            pltpu.make_async_remote_copy(
                src_ref=send.at[q, other], dst_ref=place(out, q),
                send_sem=send_sem, recv_sem=recv_sem,
                device_id=(other // n_tm, lax.rem(other, n_tm)),
                device_id_type=pl.DeviceIdType.MESH,
            ).start()
            return _

        lax.fori_loop(1, n_dev, post, 0)
        own(q).start()

    def chunk_of(k):
        return lax.rem(k + 1, chunks)

    load(0).wait()
    load(1).wait()
    each(lambda tile: fir(chunk_of(0) * CHUNK, tile, 0))

    def turn(k, carry):
        q = chunk_of(k)
        later = chunk_of(k + 1)

        def second(tile):
            fir(q * CHUNK + GROUP, tile, 1)
            dft(tile, 0)

        each(second)

        @pl.when(later > 0)
        def _():
            load(later).wait()

        @pl.when((later == 0) & (tm > 0))
        def _():
            history.wait_recv()

        def first(tile):
            fir(later * CHUNK, tile, 0)
            dft(tile, 1)

        each(first)
        dispatch(q)
        return carry

    lax.fori_loop(0, chunks - 1, turn, 0)

    def final(tile):
        fir(GROUP, tile, 1)
        dft(tile, 0)

    each(final)
    each(lambda tile: dft(tile, 1))
    dispatch(0)

    @pl.when(tm < n_tm - 1)
    def _():
        history.wait_send()

    sent = send.at[:, pl.ds(0, n_dev - 1)]
    pltpu.make_async_copy(sent, sent, send_sem).wait()
    pltpu.make_async_copy(out, out, recv_sem).wait()


def correlate_kernel(z_ref, o_ref, wide, turned, crossed):
    groups, _, spectra, in_rows = z_ref.shape
    block = o_ref.shape[2]

    @pl.when(pl.program_id(0) == 0)
    def _():
        for g in range(groups):
            cols = slice(g * in_rows, (g + 1) * in_rows)
            for p in range(2):
                part = z_ref[g, p]
                wide[p * spectra : (p + 1) * spectra, cols] = part
                flip = part.T
                turned[cols, p * spectra : (p + 1) * spectra] = flip
                crossed[cols, (1 - p) * spectra : (2 - p) * spectra] = flip if p else -flip

    rows = pl.ds(pl.multiple_of(pl.program_id(0) * block, block), block)
    scale = 1.0 / spectra
    o_ref[0, 0] = jnp.dot(turned[rows, :], wide[...], preferred_element_type=jnp.float32) * scale
    o_ref[0, 1] = jnp.dot(crossed[rows, :], wide[...], preferred_element_type=jnp.float32) * scale


def per_device(voltages, pfb_coeff):
    n_inp = lax.axis_size("inp")
    n_tm = lax.axis_size("tm")
    channels = n_inp * n_tm
    in_rows = voltages.shape[0]
    taps, length = pfb_coeff.shape
    spec = voltages.shape[1] // length
    lines = 2 * channels
    table = jnp.asarray(dft_tables(channels, length))
    vmem = pl.BlockSpec(memory_space=pltpu.VMEM)
    hbm = pl.BlockSpec(memory_space=pl.ANY)
    bf16 = jnp.bfloat16
    received = pl.pallas_call(
        functools.partial(channelize_kernel, n_inp, n_tm),
        out_shape=jax.ShapeDtypeStruct((n_inp, 2, n_tm * spec, in_rows), bf16),
        in_specs=[hbm, vmem, vmem],
        out_specs=hbm,
        scratch_shapes=[
            pltpu.VMEM((in_rows, (spec + taps - 1) * length), bf16),
            pltpu.VMEM((taps, 8, length), jnp.float32),
            pltpu.VMEM((2, GROUP, in_rows, length), bf16),
            pltpu.VMEM((2, GROUP, in_rows, length), bf16),
            pltpu.VMEM((lines * CHUNK, in_rows), jnp.float32),
            pltpu.VMEM((spec // CHUNK, channels, 2, CHUNK, in_rows), bf16),
            pltpu.SemaphoreType.DMA((spec // CHUNK,)),
            pltpu.SemaphoreType.DMA,
            pltpu.SemaphoreType.DMA,
            pltpu.SemaphoreType.DMA,
            pltpu.SemaphoreType.DMA,
        ],
        compiler_params=pltpu.CompilerParams(
            collective_id=0, has_side_effects=True, vmem_limit_bytes=60 * 1024 * 1024
        ),
        name="channelize",
    )(voltages, pfb_coeff, table)
    inputs = n_inp * in_rows
    spectra = n_tm * spec
    block = min(256, inputs)
    return pl.pallas_call(
        correlate_kernel,
        grid=(inputs // block,),
        out_shape=jax.ShapeDtypeStruct((1, 2, inputs, inputs), jnp.float32),
        in_specs=[pl.BlockSpec(received.shape, lambda i: (0, 0, 0, 0))],
        out_specs=pl.BlockSpec((1, 2, block, inputs), lambda i: (0, 0, i, 0)),
        scratch_shapes=[
            pltpu.VMEM((2 * spectra, inputs), bf16),
            pltpu.VMEM((inputs, 2 * spectra), bf16),
            pltpu.VMEM((inputs, 2 * spectra), bf16),
        ],
        compiler_params=pltpu.CompilerParams(vmem_limit_bytes=60 * 1024 * 1024),
        name="correlate",
    )(received)


def solution(mesh):
    return jax.shard_map(
        per_device,
        mesh=mesh,
        in_specs=(P("inp", "tm"), P()),
        out_specs=P(("inp", "tm"), None, None, None),
        check_vma=False,
    )
```

time: 310 us -> 102 us (0.33)
  other arithmetic: 109 us -> 0 us
  Pallas kernels: 0 us -> 102 us
  blocking collectives: 83.7 us -> 0 us
  local copies, waits for them, and re-layouts: 67.2 us -> 0 us
  matrix products: 43.5 us -> 0 us
  starting transfers between devices: 3.69 us -> 0 us
    pallas_call x0 -> x2, Pallas kernels: none -> 102 us  [the longest x1 92.8 us: per_device(): pl.pallas_call(functools.partial(channelize_kernel, n_inp, n_tm), out_sha...]
    add x1 -> x0, other arithmetic: 91.2 us -> none  [per_device(): filtered + pfb_coeff[tap_index][None, None, :] * extended[:, tap_index:ta...]
    all_to_all x2 -> x0, blocking collectives: 83.7 us -> none  [the longest x1 49 us: per_device(): lax.all_to_all(outgoing, 'inp', split_axis=0, concat_axis=2, tiled=True)]
    dot_general x2 -> x0, matrix products: 43.5 us -> none  [the longest x1 35.3 us: per_device(): jnp.einsum('cn,asn->cas', dft_table, filtered, precision=lax.Precision.HI...]
    add x1 -> x0, local copies, waits for them, and re-layouts: 34.6 us -> none  [per_device(): filtered + pfb_coeff[tap_index][None, None, :] * extended[:, tap_index:ta...]
    unnamed x3 -> x0, local copies, waits for them, and re-layouts: 22.4 us -> none
    another operation x2 -> x0, other arithmetic: 10.3 us -> none  [the longest x1 10.3 us: correlate(): return jnp.stack([real_sum, imag_diff], axis=1) * (1.0 / spectra_all)]
    mul x2 -> x0, other arithmetic: 7.3 us -> none  [the longest x1 7.02 us: correlate(): return jnp.stack([real_sum, imag_diff], axis=1) * (1.0 / spectra_all)]
  transfers between devices with their start and end apart: 1 -> 0, of which waited for: 1 -> 0; matrix products, arithmetic and copies ran while one was open for 0% -> 0% of each run, Pallas kernels for 0% -> 0%
where the time goes in v1:
time: 102 us
  Pallas kernels  102 us (100%)
    pallas_call x1, Pallas kernels, per_device(): pl.pallas_call(functools.partial(channelize_kernel, n_inp, n_tm), out_sha...  92.8 us
    pallas_call x1, Pallas kernels, per_device(): pl.pallas_call(correlate_kernel, grid=(inputs // block,), out_shape=jax.S...  9.01 us

profile of v1, /device:TPU:0, one launch (start us, length us, event | category | flops | bytes accessed | tf_op | source)
XLA Modules:
  0.0 101.8 jit_solution(7479482278905515568)
XLA Ops:
  0.0 92.8 %channelize.1.z_ref = bf16[8,2,512,128]{3,2,1,0:T(8,128)(2,1)} custom-call(bf16[128,65536]{1,0:T(8,128)(2,1)} %volt.1, f32[16,512]{1,0:T(8,128)} %coef_in.1, bf16[128,512]{1,0:T(8,128)(2,1)} %constant.2.clone.table), custom_call_target="tpu_custom_call" | custom-call | tf_op jit(solution)/shard_map/channelize/pallas_call | solution.py:248
  92.8 9.0 %correlate.1 = f32[1,2,1024,1024]{3,2,1,0:T(8,128)} custom-call(bf16[8,2,512,128]{3,2,1,0:T(8,128)(2,1)} %channelize.1.z_ref), custom_call_target="tpu_custom_call" | custom-call | tf_op jit(solution)/shard_map/correlate/pallas_call | solution.py:274

commit v2 on v1

--- a/solution.py
+++ b/solution.py
@@ -28,7 +28,7 @@
 
 def channelize_kernel(
     n_inp, n_tm, volt, coef_in, table, out,
-    slab, coef, f_high, f_low, stage, send,
+    slab, coef, high0, low0, high1, low1, stage, send,
     load_sem, tail_send, tail_recv, send_sem, recv_sem,
 ):
     in_rows = volt.shape[0]
@@ -51,8 +51,8 @@
             load_sem.at[q],
         )
 
-    for q in range(chunks):
-        load(q).start()
+    load(0).start()
+    load(1).start()
 
     barrier = pltpu.get_barrier_semaphore()
 
@@ -67,20 +67,6 @@
     lax.fori_loop(1, n_dev, greet, 0)
     for j in range(taps):
         coef[j] = jnp.broadcast_to(coef_in[j : j + 1, :], (8, length))
-    pl.semaphore_wait(barrier, n_dev - 1)
-
-    history = pltpu.make_async_remote_copy(
-        src_ref=volt.at[:, pl.ds(spec * length - tail, tail)],
-        dst_ref=slab.at[:, pl.ds(0, tail)],
-        send_sem=tail_send, recv_sem=tail_recv,
-        device_id=(inp, lax.rem(tm + 1, n_tm)),
-        device_id_type=pl.DeviceIdType.MESH,
-    )
-
-    @pl.when(tm < n_tm - 1)
-    def _():
-        history.start()
-
     @pl.when(tm == 0)
     def _():
         def clear(e, _):
@@ -90,6 +76,8 @@
             return _
 
         lax.fori_loop(0, taps - 1, clear, 0)
+
+    f_high, f_low = (high0, high1), (low0, low1)
 
     def fir(first, tile, slot):
         row = pl.multiple_of(tile * ROWS, ROWS)
@@ -112,8 +100,8 @@
                 if i >= 0:
                     f = jnp.concatenate([low[i], high[i]], axis=0)
                     h = f.astype(jnp.bfloat16)
-                    f_high[slot, i, pl.ds(row, ROWS), lanes] = h
-                    f_low[slot, i, pl.ds(row, ROWS), lanes] = (
+                    f_high[slot][i, pl.ds(row, ROWS), lanes] = h
+                    f_low[slot][i, pl.ds(row, ROWS), lanes] = (
                         f - h.astype(jnp.float32)
                     ).astype(jnp.bfloat16)
 
@@ -121,8 +109,8 @@
         per = GROUP // a_tiles
         for u in range(per):
             i = tile * per + u
-            r = lax.dot_general(table[...], f_high[slot, i], NT, preferred_element_type=jnp.float32)
-            r2 = lax.dot_general(table[:lines], f_low[slot, i], NT, preferred_element_type=jnp.float32)
+            r = lax.dot_general(table[...], f_high[slot][i], NT, preferred_element_type=jnp.float32)
+            r2 = lax.dot_general(table[:lines], f_low[slot][i], NT, preferred_element_type=jnp.float32)
             stage[pl.ds(slot * GROUP + i, lines, stride=CHUNK), :] = r[:lines] + r[lines:] + r2
 
     def each(body):
@@ -165,15 +153,30 @@
 
     load(0).wait()
     load(1).wait()
+    for q in range(2, chunks):
+        load(q).start()
     each(lambda tile: fir(chunk_of(0) * CHUNK, tile, 0))
+    pl.semaphore_wait(barrier, n_dev - 1)
+
+    history = pltpu.make_async_remote_copy(
+        src_ref=volt.at[:, pl.ds(spec * length - tail, tail)],
+        dst_ref=slab.at[:, pl.ds(0, tail)],
+        send_sem=tail_send, recv_sem=tail_recv,
+        device_id=(inp, lax.rem(tm + 1, n_tm)),
+        device_id_type=pl.DeviceIdType.MESH,
+    )
+
+    @pl.when(tm < n_tm - 1)
+    def _():
+        history.start()
 
     def turn(k, carry):
         q = chunk_of(k)
         later = chunk_of(k + 1)
 
         def second(tile):
+            dft(tile, 0)
             fir(q * CHUNK + GROUP, tile, 1)
-            dft(tile, 0)
 
         each(second)
 
@@ -186,8 +189,8 @@
             history.wait_recv()
 
         def first(tile):
+            dft(tile, 1)
             fir(later * CHUNK, tile, 0)
-            dft(tile, 1)
 
         each(first)
         dispatch(q)
@@ -196,8 +199,8 @@
     lax.fori_loop(0, chunks - 1, turn, 0)
 
     def final(tile):
+        dft(tile, 0)
         fir(GROUP, tile, 1)
-        dft(tile, 0)
 
     each(final)
     each(lambda tile: dft(tile, 1))
@@ -253,8 +256,10 @@
         scratch_shapes=[
             pltpu.VMEM((in_rows, (spec + taps - 1) * length), bf16),
             pltpu.VMEM((taps, 8, length), jnp.float32),
-            pltpu.VMEM((2, GROUP, in_rows, length), bf16),
-            pltpu.VMEM((2, GROUP, in_rows, length), bf16),
+            pltpu.VMEM((GROUP, in_rows, length), bf16),
+            pltpu.VMEM((GROUP, in_rows, length), bf16),
+            pltpu.VMEM((GROUP, in_rows, length), bf16),
+            pltpu.VMEM((GROUP, in_rows, length), bf16),
             pltpu.VMEM((lines * CHUNK, in_rows), jnp.float32),
             pltpu.VMEM((spec // CHUNK, channels, 2, CHUNK, in_rows), bf16),
             pltpu.SemaphoreType.DMA((spec // CHUNK,)),

time: 102 us -> 81.5 us (0.80)
  Pallas kernels: 102 us -> 81.3 us
    pallas_call x1, Pallas kernels: 92.8 us -> 72.3 us  [per_device(): pl.pallas_call(functools.partial(channelize_kernel, n_inp, n_tm), out_sha...]
where the time goes in v2:
time: 81.5 us; the launch traced here: 81.3 us
  Pallas kernels  81.3 us (100%)
    pallas_call x1, Pallas kernels, per_device(): pl.pallas_call(functools.partial(channelize_kernel, n_inp, n_tm), out_sha...  72.3 us
    pallas_call x1, Pallas kernels, per_device(): pl.pallas_call(correlate_kernel, grid=(inputs // block,), out_shape=jax.S...  9.01 us

profile of v2, /device:TPU:0, one launch (start us, length us, event | category | flops | bytes accessed | tf_op | source)
XLA Modules:
  0.0 81.3 jit_solution(5065372954715691785)
XLA Ops:
  0.0 72.3 %channelize.1.z_ref = bf16[8,2,512,128]{3,2,1,0:T(8,128)(2,1)} custom-call(bf16[128,65536]{1,0:T(8,128)(2,1)} %volt.1, f32[16,512]{1,0:T(8,128)} %coef_in.1, bf16[128,512]{1,0:T(8,128)(2,1)} %constant.2.clone.table), custom_call_target="tpu_custom_call" | custom-call | tf_op jit(solution)/shard_map/channelize/pallas_call | solution.py:251
  72.3 9.0 %correlate.1 = f32[1,2,1024,1024]{3,2,1,0:T(8,128)} custom-call(bf16[8,2,512,128]{3,2,1,0:T(8,128)(2,1)} %channelize.1.z_ref), custom_call_target="tpu_custom_call" | custom-call | tf_op jit(solution)/shard_map/correlate/pallas_call | solution.py:279
